TPU v7x, 32 devices: a whole 2x2x4 slice. The times are simulated.
32 devices in a mesh: aux: 8 (over y, x, core), pair: 4 (over z).
Axes of the slice: x: 2, y: 2, z: 4, core: 2. Of those that a mesh axis runs over, the one named last changes fastest.
Arguments:
- integrals: bfloat16 [3072, 32768], P('aux', 'pair'), may hold values from -0.15625 to 0.15625
- densities: bfloat16 [16, 32768], P(None, 'pair'), may hold values from -2.390625 to 2.390625
- screen: int32 [24, 256], P('aux', 'pair'), may hold values 0 or 1
- factor: float32 [3072, 3072], P('aux', 'pair'), may hold values from -0.109375 to 0.109375
- diag_inv: float32 [3072, 768], P('aux'), may hold values from -2 to 2, as said below
Outputs:
- coulomb: float32 [16, 32768], P(None, ('pair', 'aux'))
Inputs may be any that keep to these rules, and one draw needn't show every extreme that they name: `diag_inv`: each block of 768 rows is an upper triangular matrix with a positive diagonal.
All inputs are finite; a program needn't handle non-finite values. No bound on the sum of `screen` on one device may be relied on, other than what follows from the above.
Results may differ from a plain program's by a relative error of at most 0.0041.
Values may be sent and summed in bfloat16 or wider, within the bound.
A program may use at most 128 MiB of HBM per device.

v0:
```python
import jax
import jax.numpy as jnp
from jax import lax
from jax.sharding import PartitionSpec as P

TILE = 128
SOLVE_BLOCKS = 4


def shards(integrals, densities, screen, factor, diag_inv):
    height = integrals.shape[0]
    breadth = factor.shape[1]
    block_size = diag_inv.shape[1]
    rows_aux = lax.axis_size("aux")
    total = height * rows_aux
    members = rows_aux // SOLVE_BLOCKS
    my_row = lax.axis_index("aux")
    my_column = lax.axis_index("pair")
    my_block = my_row // members
    count = densities.shape[0]
    highest = lax.Precision.HIGHEST
    expanded = jnp.repeat(jnp.repeat(screen, TILE, axis=0), TILE, axis=1).astype(jnp.bfloat16)
    masked = integrals * expanded
    partial_fit = lax.dot_general(
        densities, masked, (((1,), (1,)), ((), ())), preferred_element_type=jnp.float32
    )
    column_block = (my_column * breadth + jnp.arange(breadth, dtype=jnp.int32)) // block_size
    factor_low = jnp.where((column_block < my_block)[None, :], factor, 0.0)

    def apply_inverse(values):
        return jnp.dot(values, diag_inv, precision=highest, preferred_element_type=jnp.float32)

    def own_columns(whole):
        return lax.dynamic_slice_in_dim(whole, my_column * breadth, breadth, 1)

    def times_factor(known):
        return lax.dot_general(
            known,
            factor_low,
            (((1,), (1,)), ((), ())),
            precision=highest,
            preferred_element_type=jnp.float32,
        )

    zero_block = jnp.zeros((count, block_size), jnp.float32)
    solved = jnp.zeros((count, total), jnp.float32)
    for k in range(SOLVE_BLOCKS):

        def on_group(current):
            return apply_inverse(partial_fit - times_factor(own_columns(current)))

        def off_group(current):
            return zero_block

        summand = lax.cond(my_block == k, on_group, off_group, solved)
        arrived = lax.psum(summand, ("aux", "pair"))
        solved = lax.dynamic_update_slice_in_dim(solved, arrived, k * block_size, 1)
    own_coef = jnp.zeros((count, height), jnp.float32)
    contrib = jnp.zeros((count, total), jnp.float32)
    for target in reversed(range(SOLVE_BLOCKS)):
        if target < SOLVE_BLOCKS - 1:
            portion = contrib[:, target * block_size : (target + 1) * block_size]
            behind = lax.psum(portion, ("aux", "pair"))
            settled = solved[:, target * block_size : (target + 1) * block_size] - behind
        else:
            settled = solved[:, target * block_size : (target + 1) * block_size]

        def on_group(state):
            coef = lax.dot_general(
                settled,
                diag_inv,
                (((1,), (1,)), ((), ())),
                precision=highest,
                preferred_element_type=jnp.float32,
            )
            if target > 0:
                spread_out = jnp.dot(
                    coef, factor_low, precision=highest, preferred_element_type=jnp.float32
                )
                fresh = lax.dynamic_update_slice_in_dim(
                    jnp.zeros((count, total), jnp.float32), spread_out, my_column * breadth, 1
                )
            else:
                fresh = state[1]
            return (coef, fresh)

        def keep_state(state):
            return state

        own_coef, contrib = lax.cond(my_block == target, on_group, keep_state, (own_coef, contrib))
    rounded = own_coef.astype(jnp.bfloat16)
    summand = jnp.dot(rounded, masked, preferred_element_type=jnp.float32)
    result = lax.psum_scatter(summand, "aux", scatter_dimension=1, tiled=True)
    return result


def solution(mesh):
    in_specs = (
        P("aux", "pair"),
        P(None, "pair"),
        P("aux", "pair"),
        P("aux", "pair"),
        P("aux", None),
    )
    out_specs = P(None, ("pair", "aux"))
    return jax.shard_map(shards, mesh=mesh, in_specs=in_specs, out_specs=out_specs, check_vma=False)
```

profile of v0, /device:TPU:31, one launch (start us, length us, event | category | flops | bytes accessed | tf_op | source)
XLA Modules:
  0.0 367.6 jit_solution(1663735948647780986)
XLA Ops:
  6.5 0.0 copy-start
  6.5 0.0 reduce-scatter.2.cloned.1.call-start
  6.6 0.7 convert_element_type.40
  7.3 1.3 broadcast_select_fusion
  8.7 0.0 copy-start.3
  8.7 3.8 %broadcast_in_dim.25 = bf16[384,64,128]{2,1,0:T(8,128)(2,1)S(1)} broadcast(bf16[384,64]{1,0:T(8,128)(2,1)S(1)} %bitcast.36), dimensions={0,1} | broadcast | bytes 6340608 | tf_op jit(solution)/shard_map/broadcast_in_dim | solution.py:22
  12.5 0.0 copy-start.2
  12.5 0.0 copy-done
  12.5 0.0 copy-done.3
  12.5 0.0 copy-start.1
  12.6 4.0 %fusion.18 = f32[16,384]{1,0:T(8,128)S(1)} fusion(bf16[16,8192]{1,0:T(8,128)(2,1)S(1)} %copy-done, bf16[384,8192]{1,0:T(8,128)(2,1)S(1)} %copy-done.3, bf16[48,8,64,128]{3,2,1,0:T(8,128)(2,1)S(1)} %bitcast.34), kind=kOutput, calls=%fused_computation.26 | convolution fusion | flops 103809024 | bytes 12869632 | tf_op jit(solution)/shard_map/dot_general | solution.py:24
  16.5 0.0 copy-done.2
  16.5 0.0 copy-done.1
  16.6 39.3 %psum.49 = f32[16,768]{1,0:T(8,128)S(1)} all-reduce(f32[16,768]{1,0:T(8,128)S(1)} %get-tuple-element.168), channel_id=1, replica_groups=mesh['aux'=8,'pair'=4] {'aux','pair'}, use_global_device_ids=true, to_apply=%region_2.3 | all-reduce | flops 12288 | bytes 98304 | tf_op jit(solution)/shard_map/psum | solution.py:56
  55.9 41.7 %psum.50 = f32[16,768]{1,0:T(8,128)S(1)} all-reduce(f32[16,768]{1,0:T(8,128)S(1)} %get-tuple-element.169), channel_id=1, replica_groups=mesh['aux'=8,'pair'=4] {'aux','pair'}, use_global_device_ids=true, to_apply=%region_5.6 | all-reduce | flops 12288 | bytes 98304 | tf_op jit(solution)/shard_map/psum | solution.py:56
  97.7 40.7 %psum.51 = f32[16,768]{1,0:T(8,128)S(1)} all-reduce(f32[16,768]{1,0:T(8,128)S(1)} %get-tuple-element.170), channel_id=1, replica_groups=mesh['aux'=8,'pair'=4] {'aux','pair'}, use_global_device_ids=true, to_apply=%region_8.9 | all-reduce | flops 12288 | bytes 98304 | tf_op jit(solution)/shard_map/psum | solution.py:56
  138.4 2.0 conditional.11
  138.6 1.1 convolution_subtract_fusion.3
  139.7 0.7 fusion.25
  140.3 41.7 %psum.52 = f32[16,768]{1,0:T(8,128)S(1)} all-reduce(f32[16,768]{1,0:T(8,128)S(1)} %get-tuple-element.171), channel_id=1, replica_groups=mesh['aux'=8,'pair'=4] {'aux','pair'}, use_global_device_ids=true, to_apply=%region_11.12 | all-reduce | flops 12288 | bytes 98304 | tf_op jit(solution)/shard_map/psum | solution.py:56
  182.1 4.5 %conditional.12 = (f32[16,384]{1,0:T(8,128)}, f32[16,3072]{1,0:T(8,128)}) conditional(s32[]{:T(128)} %convert_element_type.39, () %tuple.70, (f32[16,768]{1,0:T(8,128)S(1)}, f32[384,768]{1,0:T(8,128)S(1)}, f32[384,768]{1,0:T(8,128)S(1)}, s32[]{:T(128)}) %tuple.110), branch_computations={%region_12.13_spmd, %region_13.14_spmd} | conditional | flops 113246208 | bytes 2703430 | solution.py:90
  182.1 1.7 fusion.26
  183.8 0.7 broadcast.58
  184.5 2.0 convolution_dynamic-update-slice_fusion
  186.6 0.8 slice.19
  187.4 38.7 %psum.53 = f32[16,768]{1,0:T(8,128)S(1)} all-reduce(f32[16,768]{1,0:T(8,128)S(1)} %slice.19), channel_id=1, replica_groups=mesh['aux'=8,'pair'=4] {'aux','pair'}, use_global_device_ids=true, to_apply=%region_14.15 | all-reduce | flops 12288 | bytes 98304 | tf_op jit(solution)/shard_map/psum | solution.py:63
  226.1 0.8 slice.20
  226.9 44.5 %psum.54 = f32[16,768]{1,0:T(8,128)S(1)} all-reduce(f32[16,768]{1,0:T(8,128)S(1)} %slice.20), channel_id=1, replica_groups=mesh['aux'=8,'pair'=4] {'aux','pair'}, use_global_device_ids=true, to_apply=%region_17.18 | all-reduce | flops 12288 | bytes 98304 | tf_op jit(solution)/shard_map/psum | solution.py:63
  271.4 0.8 slice.21
  272.2 43.1 %psum.55 = f32[16,768]{1,0:T(8,128)S(1)} all-reduce(f32[16,768]{1,0:T(8,128)S(1)} %slice.21), channel_id=1, replica_groups=mesh['aux'=8,'pair'=4] {'aux','pair'}, use_global_device_ids=true, to_apply=%region_20.21 | all-reduce | flops 12288 | bytes 98304 | tf_op jit(solution)/shard_map/psum | solution.py:63
  315.3 0.2 conditional.15
  315.6 9.1 %fusion.16 = f32[16,8192]{1,0:T(8,128)} fusion(bf16[384,8192]{1,0:T(8,128)(2,1)} %param.21, bf16[48,8,64,128]{3,2,1,0:T(8,128)(2,1)} %bitcast.35, f32[16,384]{1,0:T(8,128)} %get-tuple-element.174), kind=kOutput, calls=%fused_computation.24 | convolution fusion | flops 103815168 | bytes 13131776 | tf_op jit(solution)/shard_map/dot_general | solution.py:92
  324.7 0.0 reduce-scatter.2.cloned.1.call-update
  324.7 36.1 %reduce-scatter.2.cloned.1.call-done = f32[16,1024]{1,0:T(8,128)} async-done(((f32[16,8192]{1,0:T(8,128)}), f32[16,1024]{1,0:T(8,128)}) %reduce-scatter.2.cloned.1.call-update) | async-done | bytes 65552 | tf_op jit(solution)/shard_map/reduce_scatter | solution.py:93
  (13 shorter events, 0.2 us)
Async XLA Ops:
  6.5 6.0 %copy-start = (bf16[16,8192]{1,0:T(8,128)(2,1)S(1)}, bf16[16,8192]{1,0:T(8,128)(2,1)}, u32[]{:S(2)}) copy-start(bf16[16,8192]{1,0:T(8,128)(2,1)} %param.22) | copy-start | bytes 786436
  6.5 354.2 %reduce-scatter.2.cloned.1.call-start = ((), (), s32[]{:S(2)}) async-start(), calls=%async_computation.1 | async-start | bytes 589824 | tf_op jit(solution)/shard_map/reduce_scatter | solution.py:93
  8.7 3.9 %copy-start.3 = (bf16[384,8192]{1,0:T(8,128)(2,1)S(1)}, bf16[384,8192]{1,0:T(8,128)(2,1)}, u32[]{:S(2)}) copy-start(bf16[384,8192]{1,0:T(8,128)(2,1)} %param.21) | copy-start | bytes 18874372
  12.5 4.0 %copy-start.2 = (bf16[384,64,128]{2,1,0:T(8,128)(2,1)}, bf16[384,64,128]{2,1,0:T(8,128)(2,1)S(1)}, u32[]{:S(2)}) copy-start(bf16[384,64,128]{2,1,0:T(8,128)(2,1)S(1)} %broadcast_in_dim.25) | copy-start | bytes 18874372
  12.5 4.0 %copy-start.1 = (f32[384,768]{1,0:T(8,128)S(1)}, f32[384,768]{1,0:T(8,128)}, u32[]{:S(2)}) copy-start(f32[384,768]{1,0:T(8,128)} %param.25) | copy-start | bytes 3538948
Sparse Core Ops, SparseCore 0:
  324.8 35.9 reduce-scatter.1
where the time goes:
time: 372 us; the launch traced here: 368 us
  blocking collectives  290 us (78%)
  waiting for transfers between devices  36.1 us (10%)
  matrix products  18.6 us (5%)
  between operations  13.6 us (4%)
  local copies, waits for them, and re-layouts  7.01 us (2%)
    psum x4, blocking collectives, shards(): arrived = lax.psum(summand, ('aux', 'pair'))  163 us
    psum x3, blocking collectives, shards(): behind = lax.psum(portion, ('aux', 'pair'))  126 us
    reduce_scatter x1, waiting for transfers between devices, shards(): result = lax.psum_scatter(summand, 'aux', scatter_dimension=1, tiled=True)  36.1 us
    dot_general x1, matrix products, shards(): summand = jnp.dot(rounded, masked, preferred_element_type=jnp.float32)  9.1 us
  transfers between devices with their start and end apart: 1, of which 1 were waited for; matrix products, arithmetic and copies ran while one was open for 0% of the time, Pallas kernels for 0%

commit v1 on v0

v1 whole, which is shorter than its diff:
```python
import functools

import jax
import jax.numpy as jnp
from jax import lax
from jax.experimental import pallas as pl
from jax.experimental.pallas import tpu as pltpu
from jax.sharding import PartitionSpec as P

TILE = 128
SOLVE_BLOCKS = 4
STREAM = 1024
MESH = pl.DeviceIdType.MESH
NN = (((1,), (0,)), ((), ()))
NT = (((1,), (1,)), ((), ()))
F32 = jnp.float32
BF16 = jnp.bfloat16


def split(values):
    high = values.astype(BF16)
    return high, (values - high.astype(F32)).astype(BF16)


def dot_split(values, high, low, dims):
    top, rest = split(values)
    rows = values.shape[0]
    both = lax.dot_general(
        jnp.concatenate([top, rest], 0), high, dims, preferred_element_type=F32
    )
    minor = lax.dot_general(top, low, dims, preferred_element_type=F32)
    return both[:rows] + (both[rows:] + minor)


def kernel(
    n_aux, n_pair,
    integrals, densities, screen, factor, diag_inv, out,
    masked, dens, fac, inv, fac_hi, fac_lo, inv_hi, inv_lo,
    fit_out, fit_in, u_out, u_in, s_out, s_in, s_sum, own_in, resid, coef, v_out, v_in,
    part_out, part_in,
    load_sem, small_sem,
    fit_send, fit_recv, u_send, u_recv, s_send, s_recv, own_send, own_recv,
    coef_send, coef_recv, v_send, v_recv, part_send, part_recv,
):
    height, width = masked.shape
    breadth = fac.shape[1]
    block = inv.shape[1]
    members = block // height
    group = block // breadth
    pieces = breadth // height
    share = width // n_aux
    chunks = width // STREAM

    row = lax.axis_index("aux")
    col = lax.axis_index("pair")
    mine = row // members
    member = lax.rem(row, members)
    column_block = col // group
    column_part = lax.rem(col, group)

    def home_of(k):
        return jnp.maximum(k - 1, 0) * group

    home = home_of(mine)
    is_home = col == home
    below = column_block < mine

    def remote(src, dst, send, recv, aux, pair):
        return pltpu.make_async_remote_copy(
            src_ref=src, dst_ref=dst, send_sem=send, recv_sem=recv,
            device_id={"aux": aux, "pair": pair}, device_id_type=MESH,
        )

    def load(c):
        at = pl.ds(pl.multiple_of(c * STREAM, STREAM), STREAM)
        return pltpu.make_async_copy(integrals.at[:, at], masked.at[:, at], load_sem.at[c])

    load_dens = pltpu.make_async_copy(densities, dens, small_sem.at[0])
    load_fac = pltpu.make_async_copy(factor, fac, small_sem.at[1])
    load_inv = pltpu.make_async_copy(diag_inv, inv, small_sem.at[2])
    load_dens.start()
    for c in range(chunks):
        load(c).start()
    load_inv.start()

    @pl.when(below)
    def _():
        load_fac.start()

    barrier = pltpu.get_barrier_semaphore()
    everyone = n_aux * n_pair
    me = row * n_pair + col

    def greet(i, carry):
        other = lax.rem(me + i, everyone)
        pl.semaphore_signal(
            barrier, inc=1,
            device_id={"aux": other // n_pair, "pair": lax.rem(other, n_pair)},
            device_id_type=MESH,
        )
        return carry

    lax.fori_loop(1, everyone, greet, 0)
    load_dens.wait()

    def fit_step(c, total):
        load(c).wait()
        base = pl.multiple_of(c * STREAM, STREAM)
        for r in range(height // TILE):
            for t in range(STREAM // TILE):
                flag = screen[r, c * (STREAM // TILE) + t].astype(F32)
                at = (pl.ds(r * TILE, TILE), pl.ds(pl.multiple_of(base + t * TILE, TILE), TILE))
                masked[at] = masked[at] * jnp.full((TILE, TILE), flag, F32).astype(BF16)
        span = pl.ds(base, STREAM)
        return total + lax.dot_general(
            dens[:, span], masked[:, span], NT, preferred_element_type=F32
        )

    fitted = lax.fori_loop(0, chunks, fit_step, jnp.zeros((dens.shape[0], height), F32))
    fit_out[...] = fitted
    pl.semaphore_wait(barrier, everyone - 1)

    send_fit = remote(fit_out, fit_in.at[col], fit_send, fit_recv.at[col], row, home)

    @pl.when(jnp.logical_not(is_home))
    def _():
        send_fit.start()

    load_inv.wait()
    high, low = split(inv[...])
    inv_hi[...] = high
    inv_lo[...] = low

    @pl.when(below)
    def _():
        load_fac.wait()
        high, low = split(fac[...])
        fac_hi[...] = high
        fac_lo[...] = low

    @pl.when(below)
    def _():
        for x in range(pieces):
            whole_x = column_part * pieces + x
            for c in range(members):
                @pl.when(whole_x >= c)
                def _():
                    remote(s_out.at[0], s_in.at[c, x], s_send.at[0, 0], s_recv.at[c, x], row, col).wait_recv()
                    if c == 0:
                        s_sum[x] = s_in[c, x]
                    else:
                        s_sum[x] += s_in[c, x]
        known = jnp.concatenate([s_sum[x] for x in range(pieces)], 1)
        u_out[...] = dot_split(known, fac_hi[...], fac_lo[...], NT)

        @pl.when(jnp.logical_not(is_home))
        def _():
            remote(u_out, u_in.at[col], u_send, u_recv.at[col], row, home).start()

    def send_solved(x, start):
        part, piece = x // pieces, x % pieces

        def later(d, carry):
            copy = remote(
                s_out.at[x], s_in.at[member, piece], s_send.at[x, d],
                s_recv.at[member, piece], d, mine * group + part,
            )
            copy.start() if start else copy.wait_send()
            return carry

        lax.fori_loop((mine + 1) * members, n_aux, later, 0)
        for i in range(1, members):
            other = lax.rem(member + i, members)

            @pl.when(other <= x)
            def _():
                copy = remote(
                    s_out.at[x], own_in.at[member, x], own_send.at[x, i],
                    own_recv.at[member, x], mine * members + other, home,
                )
                copy.start() if start else copy.wait_send()

    @pl.when(is_home)
    def _():
        fit_total = fit_out
        for p in range(n_pair):
            @pl.when(p != home)
            def _():
                remote(fit_out, fit_in.at[p], fit_send, fit_recv.at[p], row, col).wait_recv()
                fit_total[...] += fit_in[p]
        for p in range(n_pair):
            @pl.when(jnp.logical_and(p // group < mine, p != home))
            def _():
                remote(u_out, u_in.at[p], u_send, u_recv.at[p], row, col).wait_recv()
                fit_total[...] -= u_in[p]

        @pl.when(below)
        def _():
            fit_total[...] -= u_out[...]

        for x in range(members):
            @pl.when(x >= member)
            def _():
                at = pl.ds(x * height, height)
                s_out[x] = dot_split(fit_total[...], inv_hi[:, at], inv_lo[:, at], NN)
                send_solved(x, True)

        for x in range(members):
            @pl.when(x >= member)
            def _():
                resid[x] = s_out[x]
                for i in range(1, members):
                    other = lax.rem(member + i, members)

                    @pl.when(other <= x)
                    def _():
                        remote(s_out.at[0], own_in.at[other, x], own_send.at[0, 0], own_recv.at[other, x], row, col).wait_recv()
                        resid[x] += own_in[other, x]

        def subtract(i, carry):
            source = n_aux - 1 - i
            for x in range(members):
                @pl.when(x >= member)
                def _():
                    remote(v_out.at[0], v_in.at[source, x], v_send.at[0, 0], v_recv.at[source, x], row, col).wait_recv()
                    resid[x] -= v_in[source, x]
            return carry

        lax.fori_loop(0, n_aux - (mine + 1) * members, subtract, 0)
        for x in reversed(range(members)):
            @pl.when(x >= member)
            def _():
                at = pl.ds(x * height, height)
                term = dot_split(resid[x], inv_hi[:, at], inv_lo[:, at], NT)
                if x == members - 1:
                    coef[...] = term
                else:
                    coef[...] += term

        for i in range(1, n_pair):
            remote(coef, coef, coef_send.at[i], coef_recv, row, lax.rem(col + i, n_pair)).start()

    @pl.when(jnp.logical_not(is_home))
    def _():
        remote(coef, coef, coef_send.at[0], coef_recv, row, col).wait_recv()

    def send_v(x, start):
        whole_x = column_part * pieces + x
        for c in range(members):
            @pl.when(c <= whole_x)
            def _():
                copy = remote(
                    v_out.at[x], v_in.at[row, whole_x], v_send.at[x, c],
                    v_recv.at[row, whole_x], column_block * members + c, home_of(column_block),
                )
                copy.start() if start else copy.wait_send()

    @pl.when(below)
    def _():
        for x in range(pieces):
            at = pl.ds(x * height, height)
            v_out[x] = dot_split(coef[...], fac_hi[:, at], fac_lo[:, at], NN)
            send_v(x, True)

    rounded = coef[...].astype(BF16)

    def product(target):
        span = pl.ds(pl.multiple_of(target * share, TILE), share)
        return lax.dot_general(rounded, masked[:, span], NN, preferred_element_type=F32)

    def part_copy(i):
        target = lax.rem(row + i, n_aux)
        return target, remote(
            part_out.at[target], part_in.at[row], part_send.at[target], part_recv.at[row], target, col
        )

    def give(i, carry):
        target, copy = part_copy(i)
        part_out[target] = product(target).astype(BF16)
        copy.start()
        return carry

    lax.fori_loop(1, n_aux, give, 0)
    total = product(row)

    def take(i, total):
        source = lax.rem(row + n_aux - i, n_aux)
        remote(part_out.at[0], part_in.at[source], part_send.at[0], part_recv.at[source], row, col).wait_recv()
        return total + part_in[source].astype(F32)

    out[...] = lax.fori_loop(1, n_aux, take, total)

    @pl.when(jnp.logical_not(is_home))
    def _():
        send_fit.wait_send()

        @pl.when(below)
        def _():
            remote(u_out, u_in.at[col], u_send, u_recv.at[col], row, home).wait_send()

    @pl.when(is_home)
    def _():
        for x in range(members):
            @pl.when(x >= member)
            def _():
                send_solved(x, False)
        for i in range(1, n_pair):
            remote(coef, coef, coef_send.at[i], coef_recv, row, lax.rem(col + i, n_pair)).wait_send()

    @pl.when(below)
    def _():
        for x in range(pieces):
            send_v(x, False)

    def sent(i, carry):
        part_copy(i)[1].wait_send()
        return carry

    lax.fori_loop(1, n_aux, sent, 0)


def shards(integrals, densities, screen, factor, diag_inv):
    n_aux, n_pair = lax.axis_size("aux"), lax.axis_size("pair")
    height, width = integrals.shape
    breadth, block = factor.shape[1], diag_inv.shape[1]
    count = densities.shape[0]
    members, pieces = block // height, breadth // height
    share = width // n_aux
    vmem, dma = pltpu.VMEM, pltpu.SemaphoreType.DMA

    def rows(*lead):
        return vmem(lead + (count, height), F32)

    return pl.pallas_call(
        functools.partial(kernel, n_aux, n_pair),
        out_shape=jax.ShapeDtypeStruct((count, share), F32),
        in_specs=[
            pl.BlockSpec(memory_space=pl.ANY),
            pl.BlockSpec(memory_space=pl.ANY),
            pl.BlockSpec(memory_space=pltpu.SMEM),
            pl.BlockSpec(memory_space=pl.ANY),
            pl.BlockSpec(memory_space=pl.ANY),
        ],
        out_specs=pl.BlockSpec(memory_space=pltpu.VMEM),
        scratch_shapes=[
            vmem((height, width), BF16), vmem((count, width), BF16),
            vmem((height, breadth), F32), vmem((height, block), F32),
            vmem((height, breadth), BF16), vmem((height, breadth), BF16),
            vmem((height, block), BF16), vmem((height, block), BF16),
            rows(), rows(n_pair), rows(), rows(n_pair),
            rows(members), rows(members, pieces), rows(pieces), rows(members, members),
            rows(members), rows(), rows(pieces), rows(n_aux, members),
            vmem((n_aux, count, share), BF16), vmem((n_aux, count, share), BF16),
            dma((width // STREAM,)), dma((3,)),
            dma, dma((n_pair,)), dma, dma((n_pair,)),
            dma((members, n_aux)), dma((members, pieces)),
            dma((members, members)), dma((members, members)),
            dma((n_pair,)), dma, dma((pieces, members)), dma((n_aux, members)),
            dma((n_aux,)), dma((n_aux,)),
        ],
        compiler_params=pltpu.CompilerParams(
            collective_id=0, has_side_effects=True, vmem_limit_bytes=60 * 2**20
        ),
    )(integrals, densities, screen, factor, diag_inv)


def solution(mesh):
    in_specs = (
        P("aux", "pair"),
        P(None, "pair"),
        P("aux", "pair"),
        P("aux", "pair"),
        P("aux", None),
    )
    out_specs = P(None, ("pair", "aux"))
    return jax.shard_map(shards, mesh=mesh, in_specs=in_specs, out_specs=out_specs, check_vma=False)
```

time: 372 us -> 54.9 us (0.15); the launches traced: 368 us -> 54.7 us
  blocking collectives: 290 us -> 0 us
  Pallas kernels: 0 us -> 53.3 us
  waiting for transfers between devices: 36.1 us -> 0 us
  matrix products: 18.6 us -> 0 us
  between operations: 13.6 us -> 0.01 us
  local copies, waits for them, and re-layouts: 7.01 us -> 1.47 us
    psum x7 -> x0, blocking collectives: 290 us -> none  [the longest x4 163 us: shards(): arrived = lax.psum(summand, ('aux', 'pair'))]
    pallas_call x0 -> x1, Pallas kernels: none -> 53.3 us  [shards(): pl.pallas_call(functools.partial(kernel, n_aux, n_pair), out_shape=jax.Sh...]
    reduce_scatter x1 -> x0, waiting for transfers between devices: 36.1 us -> none  [shards(): result = lax.psum_scatter(summand, 'aux', scatter_dimension=1, tiled=True)]
    dot_general x6 -> x0, matrix products: 18.6 us -> none  [the longest x1 9.1 us: shards(): summand = jnp.dot(rounded, masked, preferred_element_type=jnp.float32)]
    broadcast_in_dim x2 -> x0, local copies, waits for them, and re-layouts: 3.85 us -> none  [the longest x1 3.83 us: shards(): jnp.repeat(jnp.repeat(screen, TILE, axis=0), TILE, axis=1)]
  transfers between devices with their start and end apart: 1 -> 0, of which waited for: 1 -> 0; matrix products, arithmetic and copies ran while one was open for 0% -> 0% of each run, Pallas kernels for 0% -> 0%
where the time goes in v1:
time: 54.9 us; the launch traced here: 54.7 us
  Pallas kernels  53.3 us (97%)
  local copies, waits for them, and re-layouts  1.47 us (3%)
    pallas_call x1, Pallas kernels, shards(): pl.pallas_call(functools.partial(kernel, n_aux, n_pair), out_shape=jax.Sh...  53.3 us
    unnamed x1, local copies, waits for them, and re-layouts  1.47 us

profile of v1, /device:TPU:31, one launch (start us, length us, event | category | flops | bytes accessed | tf_op | source)
XLA Modules:
  0.0 54.7 jit_solution(8375380413830838263)
XLA Ops:
  0.0 53.3 %shard_map.55 = f32[16,1024]{1,0:T(8,128)} custom-call(bf16[384,8192]{1,0:T(8,128)(2,1)} %integrals.1, bf16[16,8192]{1,0:T(8,128)(2,1)} %densities.1, s32[3,64]{1,0:T(4,128)} %screen.1, f32[384,768]{1,0:T(8,128)} %factor.1, f32[384,768]{1,0:T(8,128)} %diag_inv.1), custom_call_target="tpu_custom_call" | custom-call | tf_op jit(solution)/shard_map/pallas_call | solution.py:334
  53.3 1.5 %copy.7 = f32[16,1024]{1,0:T(8,128)} copy(f32[16,1024]{1,0:T(8,128)} %shard_map.55) | data formatting | bytes 131072

commit v2 on v1

--- a/solution.py
+++ b/solution.py
@@ -10,6 +10,7 @@
 TILE = 128
 SOLVE_BLOCKS = 4
 STREAM = 1024
+VMEM_ROOM = 48 * 2**20
 MESH = pl.DeviceIdType.MESH
 NN = (((1,), (0,)), ((), ()))
 NT = (((1,), (1,)), ((), ()))
@@ -32,7 +33,7 @@
     return both[:rows] + (both[rows:] + minor)
 
 
-def kernel(
+def spread_kernel(
     n_aux, n_pair,
     integrals, densities, screen, factor, diag_inv, out,
     masked, dens, fac, inv, fac_hi, fac_lo, inv_hi, inv_lo,
@@ -319,6 +320,322 @@
     lax.fori_loop(1, n_aux, sent, 0)
 
 
+def lead_kernel(
+    n_aux, n_pair,
+    integrals, densities, screen, factor, diag_inv, out,
+    masked, dens, fac, inv, fac_hi, fac_lo, inv_hi, inv_lo, step_hi, step_lo,
+    fit_out, fit_in, u_out, u_in, s_in, s_own, resid, coef, rounded, v_out, v_in,
+    part_out, part_in,
+    load_sem, small_sem, fac_send, fac_recv, inv_send, inv_recv,
+    fit_send, fit_recv, u_send, u_recv, s_send, s_recv,
+    coef_send, coef_recv, round_send, round_recv, v_send, v_recv, part_send, part_recv,
+):
+    height, width = masked.shape
+    block = inv.shape[1]
+    members = block // height
+    share = width // n_aux
+    chunks = width // STREAM
+
+    row = lax.axis_index("aux")
+    col = lax.axis_index("pair")
+    mine = row // members
+    member = lax.rem(row, members)
+    lead = members - 1
+    lead_row = mine * members + lead
+    is_lead = member == lead
+
+    def home_of(k):
+        return jnp.maximum(k - 1, 0)
+
+    home = home_of(mine)
+    at_home = col == home
+    below = col < mine
+    lead_home = jnp.logical_and(is_lead, at_home)
+    lead_below = jnp.logical_and(is_lead, below)
+    lead_aside = jnp.logical_and(lead_below, col != home)
+
+    def remote(src, dst, send, recv, aux, pair):
+        return pltpu.make_async_remote_copy(
+            src_ref=src, dst_ref=dst, send_sem=send, recv_sem=recv,
+            device_id={"aux": aux, "pair": pair}, device_id_type=MESH,
+        )
+
+    def load(c):
+        at = pl.ds(pl.multiple_of(c * STREAM, STREAM), STREAM)
+        return pltpu.make_async_copy(integrals.at[:, at], masked.at[:, at], load_sem.at[c])
+
+    own = pl.ds(lead * height, height)
+    load_dens = pltpu.make_async_copy(densities, dens, small_sem.at[0])
+    load_fac = pltpu.make_async_copy(factor, fac.at[own], small_sem.at[1])
+    load_inv = pltpu.make_async_copy(diag_inv, inv.at[own], small_sem.at[2])
+
+    def move_fac(c):
+        return remote(factor, fac.at[pl.ds(c * height, height)], fac_send, fac_recv.at[c], lead_row, col)
+
+    def move_inv(c):
+        right = pl.ds(c * height, block - c * height)
+        return remote(
+            diag_inv.at[:, right], inv.at[pl.ds(c * height, height), right],
+            inv_send, inv_recv.at[c], lead_row, col,
+        )
+
+    barrier = pltpu.get_barrier_semaphore()
+    everyone = n_aux * n_pair
+    me = row * n_pair + col
+
+    def greet(i, carry):
+        other = lax.rem(me + i, everyone)
+        pl.semaphore_signal(
+            barrier, inc=1,
+            device_id={"aux": other // n_pair, "pair": lax.rem(other, n_pair)},
+            device_id_type=MESH,
+        )
+        return carry
+
+    lax.fori_loop(1, everyone, greet, 0)
+    load_dens.start()
+    for c in range(chunks):
+        load(c).start()
+
+    @pl.when(lead_home)
+    def _():
+        load_inv.start()
+        for c in range(1, lead):
+            inv[pl.ds(c * height, height), pl.ds(0, c * height)] = jnp.zeros((height, c * height), F32)
+
+    @pl.when(lead_below)
+    def _():
+        load_fac.start()
+
+    pl.semaphore_wait(barrier, everyone - 1)
+    for c in range(lead):
+        @pl.when(member == c)
+        def _():
+            @pl.when(at_home)
+            def _():
+                move_inv(c).start()
+
+            @pl.when(below)
+            def _():
+                move_fac(c).start()
+
+    load_dens.wait()
+
+    def fit_step(c, total):
+        load(c).wait()
+        base = pl.multiple_of(c * STREAM, STREAM)
+        for r in range(height // TILE):
+            for t in range(STREAM // TILE):
+                flag = screen[r, c * (STREAM // TILE) + t].astype(F32)
+                at = (pl.ds(r * TILE, TILE), pl.ds(pl.multiple_of(base + t * TILE, TILE), TILE))
+                masked[at] = masked[at] * jnp.full((TILE, TILE), flag, F32).astype(BF16)
+        span = pl.ds(base, STREAM)
+        return total + lax.dot_general(
+            dens[:, span], masked[:, span], NT, preferred_element_type=F32
+        )
+
+    fit_out[...] = lax.fori_loop(0, chunks, fit_step, jnp.zeros((dens.shape[0], height), F32))
+
+    send_fit = remote(
+        fit_out, fit_in.at[col, member], fit_send, fit_recv.at[col, member], lead_row, home
+    )
+
+    @pl.when(jnp.logical_not(lead_home))
+    def _():
+        send_fit.start()
+
+    @pl.when(lead_home)
+    def _():
+        load_inv.wait()
+        for c in range(lead):
+            move_inv(c).wait_recv()
+        inv_hi[...], inv_lo[...] = split(inv[...])
+
+    @pl.when(lead_below)
+    def _():
+        load_fac.wait()
+        for c in range(lead):
+            move_fac(c).wait_recv()
+
+    @pl.when(lead_aside)
+    def _():
+        fac_hi[...], fac_lo[...] = split(fac[...])
+
+    @pl.when(jnp.logical_and(lead_home, below))
+    def _():
+        high, low = split(fac[...].T)
+        fac_hi[...] = high
+        fac_lo[...] = low
+        whole = lax.dot_general(fac_hi[...], inv_hi[...], NN, preferred_element_type=F32)
+        whole += lax.dot_general(fac_lo[...], inv_hi[...], NN, preferred_element_type=F32)
+        whole += lax.dot_general(fac_hi[...], inv_lo[...], NN, preferred_element_type=F32)
+        step_hi[...], step_lo[...] = split(whole)
+
+    recv_s = remote(s_own, s_in, s_send.at[0], s_recv, row, col)
+
+    @pl.when(lead_aside)
+    def _():
+        recv_s.wait_recv()
+        u_out[...] = dot_split(s_in[...], fac_hi[...], fac_lo[...], NT)
+        remote(u_out, u_in.at[col], u_send, u_recv.at[col], row, home).start()
+
+    def send_solved(start):
+        def later(k, carry):
+            copy = remote(s_own, s_in, s_send.at[k], s_recv, k * members + lead, mine)
+            copy.start() if start else copy.wait_send()
+            return carry
+
+        lax.fori_loop(mine + 1, SOLVE_BLOCKS, later, 0)
+
+    def send_rounded(start):
+        for c in range(members):
+            for i in range(n_pair):
+                def one():
+                    copy = remote(
+                        rounded.at[c], rounded.at[c], round_send.at[c, i], round_recv,
+                        mine * members + c, lax.rem(col + i, n_pair),
+                    )
+                    copy.start() if start else copy.wait_send()
+
+                if c != lead or i:
+                    one()
+
+    def send_coef(start):
+        for p in range(n_pair):
+            @pl.when(p < mine - 1)
+            def _():
+                copy = remote(coef, coef, coef_send.at[p], coef_recv, row, p)
+                copy.start() if start else copy.wait_send()
+
+    send_v = remote(
+        v_out, v_in.at[mine], v_send, v_recv.at[mine], col * members + lead, home_of(col)
+    )
+
+    @pl.when(lead_home)
+    def _():
+        resid[:, own] = fit_out[...]
+        for p in range(n_pair):
+            for c in range(members):
+                if c != lead:
+                    @pl.when(p == home)
+                    def _():
+                        remote(fit_out, fit_in.at[p, c], fit_send, fit_recv.at[p, c], row, col).wait_recv()
+                        resid[:, pl.ds(c * height, height)] = fit_in[p, c]
+        for p in range(n_pair):
+            for c in range(members):
+                @pl.when(p != home)
+                def _():
+                    remote(fit_out, fit_in.at[p, c], fit_send, fit_recv.at[p, c], row, col).wait_recv()
+                    resid[:, pl.ds(c * height, height)] += fit_in[p, c]
+        for p in range(n_pair):
+            @pl.when(p < mine - 1)
+            def _():
+                remote(u_out, u_in.at[p], u_send, u_recv.at[p], row, col).wait_recv()
+                resid[...] -= u_in[p]
+        s_own[...] = dot_split(resid[...], inv_hi[...], inv_lo[...], NN)
+
+        @pl.when(below)
+        def _():
+            recv_s.wait_recv()
+            s_own[...] -= dot_split(s_in[...], step_hi[...], step_lo[...], NN)
+
+        send_solved(True)
+
+        resid[...] = s_own[...]
+
+        def subtract(i, carry):
+            source = SOLVE_BLOCKS - 1 - i
+            remote(v_out, v_in.at[source], v_send, v_recv.at[source], row, col).wait_recv()
+            resid[...] -= v_in[source]
+            return carry
+
+        lax.fori_loop(0, SOLVE_BLOCKS - 1 - mine, subtract, 0)
+
+        @pl.when(below)
+        def _():
+            v_out[...] = dot_split(resid[...], step_hi[...], step_lo[...], NT)
+            send_v.start()
+
+        coef[...] = dot_split(resid[...], inv_hi[...], inv_lo[...], NT)
+        for c in range(members):
+            rounded[c] = coef[:, pl.ds(c * height, height)].astype(BF16)
+        send_coef(True)
+        send_rounded(True)
+
+    @pl.when(lead_aside)
+    def _():
+        remote(coef, coef, coef_send.at[0], coef_recv, row, col).wait_recv()
+        v_out[...] = dot_split(coef[...], fac_hi[...], fac_lo[...], NN)
+        send_v.start()
+
+    @pl.when(jnp.logical_not(lead_home))
+    def _():
+        remote(rounded.at[0], rounded.at[0], round_send.at[0, 0], round_recv, row, col).wait_recv()
+
+    mine_rounded = rounded[member]
+
+    def product(target):
+        span = pl.ds(pl.multiple_of(target * share, TILE), share)
+        return lax.dot_general(mine_rounded, masked[:, span], NN, preferred_element_type=F32)
+
+    def part_copy(i):
+        target = lax.rem(row + i, n_aux)
+        return target, remote(
+            part_out.at[target], part_in.at[row], part_send.at[target], part_recv.at[row], target, col
+        )
+
+    def give(i, carry):
+        target, copy = part_copy(i)
+        part_out[target] = product(target).astype(BF16)
+        copy.start()
+        return carry
+
+    lax.fori_loop(1, n_aux, give, 0)
+    total = product(row)
+
+    def take(i, total):
+        source = lax.rem(row + n_aux - i, n_aux)
+        remote(part_out.at[0], part_in.at[source], part_send.at[0], part_recv.at[source], row, col).wait_recv()
+        return total + part_in[source].astype(F32)
+
+    out[...] = lax.fori_loop(1, n_aux, take, total)
+
+    for c in range(lead):
+        @pl.when(member == c)
+        def _():
+            @pl.when(at_home)
+            def _():
+                move_inv(c).wait_send()
+
+            @pl.when(below)
+            def _():
+                move_fac(c).wait_send()
+
+    @pl.when(jnp.logical_not(lead_home))
+    def _():
+        send_fit.wait_send()
+
+    @pl.when(lead_aside)
+    def _():
+        remote(u_out, u_in.at[col], u_send, u_recv.at[col], row, home).wait_send()
+
+    @pl.when(lead_below)
+    def _():
+        send_v.wait_send()
+
+    @pl.when(lead_home)
+    def _():
+        send_solved(False)
+        send_coef(False)
+        send_rounded(False)
+
+    def sent(i, carry):
+        part_copy(i)[1].wait_send()
+        return carry
+
+    lax.fori_loop(1, n_aux, sent, 0)
+
+
 def shards(integrals, densities, screen, factor, diag_inv):
     n_aux, n_pair = lax.axis_size("aux"), lax.axis_size("pair")
     height, width = integrals.shape
@@ -331,18 +648,28 @@
     def rows(*lead):
         return vmem(lead + (count, height), F32)
 
-    return pl.pallas_call(
-        functools.partial(kernel, n_aux, n_pair),
-        out_shape=jax.ShapeDtypeStruct((count, share), F32),
-        in_specs=[
-            pl.BlockSpec(memory_space=pl.ANY),
-            pl.BlockSpec(memory_space=pl.ANY),
-            pl.BlockSpec(memory_space=pltpu.SMEM),
-            pl.BlockSpec(memory_space=pl.ANY),
-            pl.BlockSpec(memory_space=pl.ANY),
-        ],
-        out_specs=pl.BlockSpec(memory_space=pltpu.VMEM),
-        scratch_shapes=[
+    def whole(*lead):
+        return vmem(lead + (count, block), F32)
+
+    weights = 2 * block * block * 4 + 6 * block * block * 2
+    if breadth == block and weights + integrals.size * 2 <= VMEM_ROOM:
+        body = lead_kernel
+        scratch = [
+            vmem((height, width), BF16), vmem((count, width), BF16),
+            vmem((block, block), F32), vmem((block, block), F32),
+            *[vmem((block, block), BF16) for _ in range(6)],
+            rows(), rows(n_pair, members), whole(), whole(n_pair), whole(), whole(), whole(), whole(),
+            vmem((members, count, height), BF16), whole(), whole(SOLVE_BLOCKS),
+            vmem((n_aux, count, share), BF16), vmem((n_aux, count, share), BF16),
+            dma((width // STREAM,)), dma((3,)),
+            dma, dma((members,)), dma, dma((members,)),
+            dma, dma((n_pair, members)), dma, dma((n_pair,)), dma((SOLVE_BLOCKS,)), dma,
+            dma((n_pair,)), dma, dma((members, n_pair)), dma, dma, dma((SOLVE_BLOCKS,)),
+            dma((n_aux,)), dma((n_aux,)),
+        ]
+    else:
+        body = spread_kernel
+        scratch = [
             vmem((height, width), BF16), vmem((count, width), BF16),
             vmem((height, breadth), F32), vmem((height, block), F32),
             vmem((height, breadth), BF16), vmem((height, breadth), BF16),
@@ -357,7 +684,19 @@
             dma((members, members)), dma((members, members)),
             dma((n_pair,)), dma, dma((pieces, members)), dma((n_aux, members)),
             dma((n_aux,)), dma((n_aux,)),
+        ]
+    return pl.pallas_call(
+        functools.partial(body, n_aux, n_pair),
+        out_shape=jax.ShapeDtypeStruct((count, share), F32),
+        in_specs=[
+            pl.BlockSpec(memory_space=pl.ANY),
+            pl.BlockSpec(memory_space=pl.ANY),
+            pl.BlockSpec(memory_space=pltpu.SMEM),
+            pl.BlockSpec(memory_space=pl.ANY),
+            pl.BlockSpec(memory_space=pl.ANY),
         ],
+        out_specs=pl.BlockSpec(memory_space=pltpu.VMEM),
+        scratch_shapes=scratch,
         compiler_params=pltpu.CompilerParams(
             collective_id=0, has_side_effects=True, vmem_limit_bytes=60 * 2**20
         ),

time: 54.9 us -> 45.2 us (0.82)
  Pallas kernels: 53.3 us -> 43.5 us
    pallas_call x1, Pallas kernels: 53.3 us -> 43.5 us  [shards(): pl.pallas_call(functools.partial(body, n_aux, n_pair), out_shape=jax.Shap...]
where the time goes in v2:
time: 45.2 us; the launch traced here: 45 us
  Pallas kernels  43.5 us (96%)
  local copies, waits for them, and re-layouts  1.47 us (3%)
    pallas_call x1, Pallas kernels, shards(): pl.pallas_call(functools.partial(body, n_aux, n_pair), out_shape=jax.Shap...  43.5 us
    unnamed x1, local copies, waits for them, and re-layouts  1.47 us

profile of v2, /device:TPU:31, one launch (start us, length us, event | category | flops | bytes accessed | tf_op | source)
XLA Modules:
  0.0 45.0 jit_solution(1131880791215632939)
XLA Ops:
  0.0 43.5 %shard_map.55 = f32[16,1024]{1,0:T(8,128)} custom-call(bf16[384,8192]{1,0:T(8,128)(2,1)} %integrals.1, bf16[16,8192]{1,0:T(8,128)(2,1)} %densities.1, s32[3,64]{1,0:T(4,128)} %screen.1, f32[384,768]{1,0:T(8,128)} %factor.1, f32[384,768]{1,0:T(8,128)} %diag_inv.1), custom_call_target="tpu_custom_call" | custom-call | tf_op jit(solution)/shard_map/pallas_call | solution.py:688
  43.5 1.5 %copy.7 = f32[16,1024]{1,0:T(8,128)} copy(f32[16,1024]{1,0:T(8,128)} %shard_map.55) | data formatting | bytes 131072

commit v3 on v2

--- a/solution.py
+++ b/solution.py
@@ -324,6 +324,7 @@
     n_aux, n_pair,
     integrals, densities, screen, factor, diag_inv, out,
     masked, dens, fac, inv, fac_hi, fac_lo, inv_hi, inv_lo, step_hi, step_lo,
+    inv_t_hi, inv_t_lo, step_t_hi, step_t_lo,
     fit_out, fit_in, u_out, u_in, s_in, s_own, resid, coef, rounded, v_out, v_in,
     part_out, part_in,
     load_sem, small_sem, fac_send, fac_recv, inv_send, inv_recv,
@@ -379,20 +380,6 @@
             inv_send, inv_recv.at[c], lead_row, col,
         )
 
-    barrier = pltpu.get_barrier_semaphore()
-    everyone = n_aux * n_pair
-    me = row * n_pair + col
-
-    def greet(i, carry):
-        other = lax.rem(me + i, everyone)
-        pl.semaphore_signal(
-            barrier, inc=1,
-            device_id={"aux": other // n_pair, "pair": lax.rem(other, n_pair)},
-            device_id_type=MESH,
-        )
-        return carry
-
-    lax.fori_loop(1, everyone, greet, 0)
     load_dens.start()
     for c in range(chunks):
         load(c).start()
@@ -407,7 +394,44 @@
     def _():
         load_fac.start()
 
-    pl.semaphore_wait(barrier, everyone - 1)
+    barrier = pltpu.get_barrier_semaphore()
+
+    def greet(aux, pair):
+        pl.semaphore_signal(
+            barrier, inc=1, device_id={"aux": aux, "pair": pair}, device_id_type=MESH
+        )
+
+    aside = jnp.logical_and(is_lead, jnp.logical_and(col >= 1, below))
+    for i in range(1, n_aux):
+        greet(lax.rem(row + i, n_aux), col)
+
+    @pl.when(lead_home)
+    def _():
+        for c in range(members):
+            for i in range(1, n_pair):
+                greet(mine * members + c, lax.rem(col + i, n_pair))
+
+    @pl.when(jnp.logical_not(at_home))
+    def _():
+        greet(lead_row, home)
+
+    for k in range(1, SOLVE_BLOCKS):
+        @pl.when(jnp.logical_and(lead_home, jnp.logical_and(mine >= 1, k > mine)))
+        def _():
+            greet(k * members + lead, mine)
+
+    @pl.when(aside)
+    def _():
+        greet(col * members + lead, home_of(col))
+
+    greeted = (
+        n_aux - 1
+        + jnp.where(lead_home, members * (n_pair - 1), 0)
+        + jnp.where(at_home, 0, 1)
+        + jnp.where(jnp.logical_and(lead_home, mine >= 1), SOLVE_BLOCKS - 1 - mine, 0)
+        + jnp.where(aside, 1, 0)
+    )
+    pl.semaphore_wait(barrier, greeted)
     for c in range(lead):
         @pl.when(member == c)
         def _():
@@ -450,6 +474,7 @@
         for c in range(lead):
             move_inv(c).wait_recv()
         inv_hi[...], inv_lo[...] = split(inv[...])
+        inv_t_hi[...], inv_t_lo[...] = split(inv[...].T)
 
     @pl.when(lead_below)
     def _():
@@ -470,6 +495,7 @@
         whole += lax.dot_general(fac_lo[...], inv_hi[...], NN, preferred_element_type=F32)
         whole += lax.dot_general(fac_hi[...], inv_lo[...], NN, preferred_element_type=F32)
         step_hi[...], step_lo[...] = split(whole)
+        step_t_hi[...], step_t_lo[...] = split(whole.T)
 
     recv_s = remote(s_own, s_in, s_send.at[0], s_recv, row, col)
 
@@ -553,10 +579,10 @@
 
         @pl.when(below)
         def _():
-            v_out[...] = dot_split(resid[...], step_hi[...], step_lo[...], NT)
+            v_out[...] = dot_split(resid[...], step_t_hi[...], step_t_lo[...], NN)
             send_v.start()
 
-        coef[...] = dot_split(resid[...], inv_hi[...], inv_lo[...], NT)
+        coef[...] = dot_split(resid[...], inv_t_hi[...], inv_t_lo[...], NN)
         for c in range(members):
             rounded[c] = coef[:, pl.ds(c * height, height)].astype(BF16)
         send_coef(True)
@@ -579,7 +605,7 @@
         return lax.dot_general(mine_rounded, masked[:, span], NN, preferred_element_type=F32)
 
     def part_copy(i):
-        target = lax.rem(row + i, n_aux)
+        target = lax.rem(row + n_aux - i, n_aux)
         return target, remote(
             part_out.at[target], part_in.at[row], part_send.at[target], part_recv.at[row], target, col
         )
@@ -594,7 +620,7 @@
     total = product(row)
 
     def take(i, total):
-        source = lax.rem(row + n_aux - i, n_aux)
+        source = lax.rem(row + i, n_aux)
         remote(part_out.at[0], part_in.at[source], part_send.at[0], part_recv.at[source], row, col).wait_recv()
         return total + part_in[source].astype(F32)
 
@@ -651,13 +677,13 @@
     def whole(*lead):
         return vmem(lead + (count, block), F32)
 
-    weights = 2 * block * block * 4 + 6 * block * block * 2
+    weights = 2 * block * block * 4 + 10 * block * block * 2
     if breadth == block and weights + integrals.size * 2 <= VMEM_ROOM:
         body = lead_kernel
         scratch = [
             vmem((height, width), BF16), vmem((count, width), BF16),
             vmem((block, block), F32), vmem((block, block), F32),
-            *[vmem((block, block), BF16) for _ in range(6)],
+            *[vmem((block, block), BF16) for _ in range(10)],
             rows(), rows(n_pair, members), whole(), whole(n_pair), whole(), whole(), whole(), whole(),
             vmem((members, count, height), BF16), whole(), whole(SOLVE_BLOCKS),
             vmem((n_aux, count, share), BF16), vmem((n_aux, count, share), BF16),

time: 45.2 us -> 43.7 us (0.967)
  the two profiles are of different devices: /device:TPU:31 before, /device:TPU:10 now
where the time goes in v3:
time: 43.7 us; the launch traced here: 43.5 us
  Pallas kernels  42 us (96%)
  local copies, waits for them, and re-layouts  1.47 us (3%)
    pallas_call x1, Pallas kernels, shards(): pl.pallas_call(functools.partial(body, n_aux, n_pair), out_shape=jax.Shap...  42 us
    unnamed x1, local copies, waits for them, and re-layouts  1.47 us

profile of v3, /device:TPU:10, one launch (start us, length us, event | category | flops | bytes accessed | tf_op | source)
XLA Modules:
  0.0 43.5 jit_solution(5839730840760236152)
XLA Ops:
  0.0 42.0 %shard_map.55 = f32[16,1024]{1,0:T(8,128)} custom-call(bf16[384,8192]{1,0:T(8,128)(2,1)} %integrals.1, bf16[16,8192]{1,0:T(8,128)(2,1)} %densities.1, s32[3,64]{1,0:T(4,128)} %screen.1, f32[384,768]{1,0:T(8,128)} %factor.1, f32[384,768]{1,0:T(8,128)} %diag_inv.1), custom_call_target="tpu_custom_call" | custom-call | tf_op jit(solution)/shard_map/pallas_call | solution.py:714
  42.0 1.5 %copy.7 = f32[16,1024]{1,0:T(8,128)} copy(f32[16,1024]{1,0:T(8,128)} %shard_map.55) | data formatting | bytes 131072
